TPU v7x, 32 devices: a whole 2x2x4 slice. The times are simulated.
32 devices in a mesh: seq: 8 (over z, x), head: 4 (over y, core).
Axes of the slice: x: 2, y: 2, z: 4, core: 2. Of those that a mesh axis runs over, the one named last changes fastest.
Arguments:
- query: bfloat16 [4096, 4096], P(('seq', 'head')), may hold values from -6 to 6
- key: bfloat16 [4096, 1024], P(('seq', 'head')), may hold values from -6 to 6
- value: bfloat16 [4096, 1024], P(('seq', 'head')), may hold values from -6 to 6
- out: bfloat16 [4096, 4096], P(('seq', 'head')), may hold values from -4 to 4
- output_gradient: bfloat16 [4096, 4096], P(('seq', 'head')), may hold values from -6 to 6
- log_sum_exp: float32 [4096, 32], P(('seq', 'head')), may hold values from 4 to 7
- segment_ids: int32 [4096], replicated, may hold values from 0 to 3, never falling along the last dimension, each value on 1 to 1536 neighbouring positions
Outputs:
- d_query: bfloat16 [4096, 4096], P(('seq', 'head'))
- key_gradient: bfloat16 [4096, 1024], P(('seq', 'head'))
- value_gradient: bfloat16 [4096, 1024], P(('seq', 'head'))
Inputs may be any that keep to these rules, and one draw needn't show every extreme that they name: `segment_ids`: never falls along the positions; a document holds at most 1536 positions, and one holds exactly 1536.
All inputs are finite; a program needn't handle non-finite values.
Results may differ from a plain program's by a relative error of at most 0.0071.
Values may be sent and summed in bfloat16 or wider, within the bound.
No kernel may reach another device: no remote copies, remote signals or barrier semaphores. Data moves between devices by JAX's collectives and lax.ppermute only.
A program may use at most 128 MiB of HBM per device.

v0:
```python
import functools
import math

import jax
import jax.numpy as jnp
from jax import lax
from jax.experimental import pallas as pl
from jax.experimental.pallas import tpu as pltpu
from jax.sharding import Mesh, PartitionSpec as P

HEAD_SIZE = 128
LONGEST = 1536
TILE_Q = 256
TILE_K = 256
LOG2E = math.log2(math.e)
GROUP = ("inner", "head")


def dot(a, b, dims):
    return lax.dot_general(a, b, (dims, ((), ())), preferred_element_type=jnp.float32)


def tile_grads(qdo_ref, stat_ref, start_ref, kv_ref, dq_t, dkv, q0, k0, key_pos, query_pos, heads):
    d = HEAD_SIZE
    factor = LOG2E / math.sqrt(d)
    rows = pl.ds(q0, TILE_Q)
    keys = pl.ds(k0, TILE_K)
    k = kv_ref[keys, :d]
    v = kv_ref[keys, d:]
    k_t = k.T
    at = key_pos + lax.broadcasted_iota(jnp.int32, (TILE_K, TILE_Q), 0)
    last = query_pos + lax.broadcasted_iota(jnp.int32, (1, TILE_Q), 1)
    allowed = (at >= start_ref[:, rows]) & (at <= last)
    grad_k = jnp.zeros((TILE_K, d), jnp.float32)
    grad_v = jnp.zeros((TILE_K, d), jnp.float32)
    for h in range(heads):
        q = qdo_ref[rows, h * d : (h + 1) * d]
        e = qdo_ref[rows, (heads + h) * d : (heads + h + 1) * d]
        scores = dot(k, q, ((1,), (1,)))
        dprobs = dot(v, e, ((1,), (1,)))
        raised = jnp.where(allowed, scores * factor - stat_ref[h : h + 1, rows], -jnp.inf)
        probs = jnp.exp2(raised)
        ds = (probs * (dprobs - stat_ref[heads + h : heads + h + 1, rows])).astype(jnp.bfloat16)
        grad_v += dot(probs.astype(jnp.bfloat16), e, ((1,), (0,)))
        grad_k += dot(ds, q, ((1,), (0,)))
        dq_t[h, :, rows] += dot(k_t, ds, ((1,), (0,)))
    dkv[keys, :d] += grad_k
    dkv[keys, d:] += grad_v


def far_kernel(low_ref, qdo_ref, stat_ref, start_ref, kv_ref, dq_t, dkv_out, dkv):
    heads, _, rows = dq_t.shape
    window = kv_ref.shape[0]
    dq_t[...] = jnp.zeros_like(dq_t)
    dkv[...] = jnp.zeros_like(dkv)

    def per_query(t, _):
        q0 = pl.multiple_of(t * TILE_Q, TILE_Q)

        def per_key(j, _):
            k0 = pl.multiple_of(j * TILE_K, TILE_K)
            tile_grads(qdo_ref, stat_ref, start_ref, kv_ref, dq_t, dkv, q0, k0, k0, window + q0, heads)
            return 0

        return lax.fori_loop(jnp.minimum(low_ref[t] // TILE_K, window // TILE_K), window // TILE_K, per_key, 0)

    lax.fori_loop(0, rows // TILE_Q, per_query, 0)
    scale = 1.0 / math.sqrt(HEAD_SIZE)
    dkv_out[:, :HEAD_SIZE] = (dkv[:, :HEAD_SIZE] * scale).astype(dkv_out.dtype)
    dkv_out[:, HEAD_SIZE:] = dkv[:, HEAD_SIZE:].astype(dkv_out.dtype)


def near_kernel(window, low_ref, qdo_ref, stat_ref, start_ref, kv_ref, dq_far, dq_out, dkv, dq_t):
    heads, d, rows = dq_far.shape
    dq_t[...] = dq_far[...]
    dkv[...] = jnp.zeros_like(dkv)
    scale = 1.0 / math.sqrt(HEAD_SIZE)

    def per_query(t, _):
        q0 = pl.multiple_of(t * TILE_Q, TILE_Q)

        def per_key(j, _):
            k0 = pl.multiple_of(j * TILE_K, TILE_K)
            tile_grads(
                qdo_ref, stat_ref, start_ref, kv_ref, dq_t, dkv, q0, k0, window + k0, window + q0, heads
            )
            return 0

        first = jnp.maximum(low_ref[t] - window, 0) // TILE_K
        lax.fori_loop(first, (q0 + TILE_Q) // TILE_K, per_key, 0)
        for h in range(heads):
            done = dq_t[h, :, pl.ds(q0, TILE_Q)] * scale
            dq_out[pl.ds(q0, TILE_Q), h * d : (h + 1) * d] = done.T.astype(dq_out.dtype)
        return 0

    lax.fori_loop(0, rows // TILE_Q, per_query, 0)
    dkv[:, :HEAD_SIZE] = dkv[:, :HEAD_SIZE] * scale


def shards(query, key, value, out, output_gradient, log_sum_exp, segment_ids):
    d = HEAD_SIZE
    tokens = query.shape[0]
    parts = lax.axis_size(GROUP)
    outers = lax.axis_size("outer")
    rows = tokens * parts
    heads = query.shape[1] // key.shape[1]
    window = LONGEST
    place = lax.axis_index("outer")

    kv = jnp.concatenate(
        [key.reshape(tokens, parts, d), value.reshape(tokens, parts, d)], axis=2
    ).transpose(1, 0, 2)
    kv = lax.all_to_all(kv, GROUP, 0, 0).reshape(rows, 2 * d)
    delta = jnp.sum(
        (output_gradient.astype(jnp.float32) * out.astype(jnp.float32)).reshape(tokens, -1, d), axis=2
    )
    stat = jnp.concatenate(
        [(log_sum_exp * LOG2E).reshape(tokens, parts, heads), delta.reshape(tokens, parts, heads)], axis=2
    ).transpose(1, 2, 0)
    stat = lax.all_to_all(stat, GROUP, 0, 0).transpose(1, 0, 2).reshape(2 * heads, rows)
    qdo = jnp.concatenate(
        [query.reshape(tokens, parts, heads * d), output_gradient.reshape(tokens, parts, heads * d)], axis=2
    ).transpose(1, 0, 2)
    qdo = lax.all_to_all(qdo, GROUP, 0, 0).reshape(rows, 2 * heads * d)

    steps = -(-window // rows)
    sizes = [min(rows, window - by * rows) for by in range(steps)]
    arrived = [
        lax.ppermute(kv[rows - sizes[by - 1] :], "outer", [(i, i + by) for i in range(outers - by)])
        for by in range(1, steps + 1)
    ]
    kv_far = jnp.concatenate(arrived[::-1], axis=0)

    padded = jnp.concatenate([jnp.full((window,), -1, segment_ids.dtype), segment_ids])
    seg_keys = lax.dynamic_slice_in_dim(padded, place * rows, window + rows, 0)
    seg_query = seg_keys[window:]
    start = jnp.sum((seg_keys[:, None] < seg_query[None, :]).astype(jnp.int32), axis=0)
    low = start[::TILE_Q]
    start = start[None, :]

    smem = pl.BlockSpec(memory_space=pltpu.SMEM)
    vmem = pl.BlockSpec(memory_space=pltpu.VMEM)
    flops = 10 * rows * d * heads
    dq_far, dkv_far = pl.pallas_call(
        far_kernel,
        out_shape=(
            jax.ShapeDtypeStruct((heads, d, rows), jnp.float32),
            jax.ShapeDtypeStruct((window, 2 * d), jnp.bfloat16),
        ),
        in_specs=[smem] + [vmem] * 4,
        out_specs=(vmem, vmem),
        scratch_shapes=[pltpu.VMEM((window, 2 * d), jnp.float32)],
        cost_estimate=pl.CostEstimate(flops=flops * 1024, bytes_accessed=1 << 22, transcendentals=0),
        name="far_grads",
    )(low, qdo, stat, start, kv_far)
    returned = []
    at = window
    for by in range(1, steps + 1):
        at -= sizes[by - 1]
        returned.append(
            lax.ppermute(
                dkv_far[at : at + sizes[by - 1]], "outer", [(i + by, i) for i in range(outers - by)]
            )
        )
    dq, dkv = pl.pallas_call(
        functools.partial(near_kernel, window),
        out_shape=(
            jax.ShapeDtypeStruct((rows, heads * d), jnp.bfloat16),
            jax.ShapeDtypeStruct((rows, 2 * d), jnp.float32),
        ),
        in_specs=[smem] + [vmem] * 5,
        out_specs=(vmem, vmem),
        scratch_shapes=[pltpu.VMEM((heads, d, rows), jnp.float32)],
        cost_estimate=pl.CostEstimate(flops=flops * 512, bytes_accessed=1 << 22, transcendentals=0),
        name="near_grads",
    )(low, qdo, stat, start, kv, dq_far)
    dq = lax.all_to_all(dq.reshape(parts, tokens, heads * d), GROUP, 0, 0)
    for by in range(1, steps + 1):
        part = returned[by - 1].astype(jnp.float32)
        dkv = dkv + jnp.pad(part, ((rows - sizes[by - 1], 0), (0, 0)))
    dkv = lax.all_to_all(dkv.astype(jnp.bfloat16).reshape(parts, tokens, 2 * d), GROUP, 0, 0)
    dkv = dkv.transpose(1, 0, 2)
    return (
        dq.transpose(1, 0, 2).reshape(tokens, -1),
        dkv[:, :, :d].reshape(tokens, -1),
        dkv[:, :, d:].reshape(tokens, -1),
    )


def solution(mesh):
    head = mesh.shape["head"]
    seq = mesh.shape["seq"]

    def run(query, key, value, out, output_gradient, log_sum_exp, segment_ids):
        inner = key.shape[1] // HEAD_SIZE // head
        finer = Mesh(mesh.devices.reshape(seq // inner, inner, head), ("outer", "inner", "head"))
        rows = P(("outer", "inner", "head"), None)
        return jax.shard_map(
            shards,
            mesh=finer,
            in_specs=(rows,) * 6 + (P(),),
            out_specs=(rows,) * 3,
            check_vma=False,
        )(query, key, value, out, output_gradient, log_sum_exp, segment_ids)

    return run
```

profile of v0, /device:TPU:0, one launch (start us, length us, event | category | flops | bytes accessed | tf_op | source)
XLA Modules:
  0.0 136.0 jit_solution(15737778657813093318)
XLA Ops:
  0.6 0.0 copy-start
  0.6 0.8 broadcast_multiply_fusion
  1.4 1.8 %multiply_bitcast_fusion = f32[16,8,32,128]{3,1,2,0:T(8,128)S(1)} fusion(bf16[128,4096]{1,0:T(8,128)(2,1)} %param.10, bf16[128,4096]{1,0:T(8,128)(2,1)} %param.11), kind=kLoop, calls=%fused_computation.2 | loop fusion | flops 1572864 | bytes 4194304
  3.2 0.4 copy.48
  3.6 0.0 copy-start.7
  3.6 0.6 reduce_sum.19
  4.2 0.0 copy-start.1
  4.2 0.0 copy-start.5
  4.2 0.1 copy.35
  4.3 0.6 maximum_bitcast_fusion.2
  4.9 5.2 %all-to-all-start.1 = ((f32[8,8,128]{2,1,0:T(8,128)}), f32[8,8,128]{2,1,0:T(8,128)S(1)}, u32[]{:S(2)}, u32[]{:S(2)}) async-start(f32[8,8,128]{2,1,0:T(8,128)} %maximum_bitcast_fusion.2), calls=%async_computation.1 | async-start | bytes 65536 | tf_op jit(solution)/shard_map/all_to_all | solution.py:120
  10.2 0.1 copy_bitcast_fusion.4
  10.3 0.9 maximum_bitcast_fusion.1
  11.1 3.8 %all-to-all-done.1 = f32[8,8,128]{2,1,0:T(8,128)S(1)} async-done(((f32[8,8,128]{2,1,0:T(8,128)}), f32[8,8,128]{2,1,0:T(8,128)S(1)}, u32[]{:S(2)}, u32[]{:S(2)}) %all-to-all-start.1) | async-done | bytes 32800 | tf_op jit(solution)/shard_map/all_to_all | solution.py:120
  14.9 3.5 %all-to-all-start.2 = ((bf16[8,128,256]{2,1,0:T(8,128)(2,1)}), bf16[8,128,256]{2,1,0:T(8,128)(2,1)S(1)}, u32[]{:S(2)}, u32[]{:S(2)}) async-start(bf16[8,128,256]{2,1,0:T(8,128)(2,1)} %maximum_bitcast_fusion.1), calls=%async_computation.2 | async-start | bytes 1048576 | tf_op jit(solution)/shard_map/all_to_all | solution.py:113
  18.4 0.2 copy_bitcast_fusion
  18.6 0.0 copy-done.9
  18.6 1.6 %maximum_bitcast_fusion = bf16[8,128,1024]{2,1,0:T(8,128)(2,1)} fusion(bf16[128,8,512]{2,0,1:T(8,128)(2,1)S(1)} %get-tuple-element.13, bf16[128,8,512]{2,0,1:T(8,128)(2,1)S(1)} %get-tuple-element.14), kind=kLoop, calls=%fused_computation.1 | loop fusion | flops 4194304 | bytes 4194304 | tf_op jit(solution)/shard_map/transpose | solution.py:123
  20.2 6.9 %all-to-all-done.2 = bf16[8,128,256]{2,1,0:T(8,128)(2,1)S(1)} async-done(((bf16[8,128,256]{2,1,0:T(8,128)(2,1)}), bf16[8,128,256]{2,1,0:T(8,128)(2,1)S(1)}, u32[]{:S(2)}, u32[]{:S(2)}) %all-to-all-start.2) | async-done | bytes 524320 | tf_op jit(solution)/shard_map/all_to_all | solution.py:113
  27.2 3.6 %all-to-all-start = ((bf16[8,128,1024]{2,1,0:T(8,128)(2,1)}), bf16[8,128,1024]{2,1,0:T(8,128)(2,1)S(1)}, u32[]{:S(2)}, u32[]{:S(2)}) async-start(bf16[8,128,1024]{2,1,0:T(8,128)(2,1)} %maximum_bitcast_fusion), calls=%async_computation | async-start | bytes 4194304 | tf_op jit(solution)/shard_map/all_to_all | solution.py:124
  30.8 3.5 %collective-permute-start.1 = (bf16[1024,256]{1,0:T(8,128)(2,1)S(1)}, bf16[1024,256]{1,0:T(8,128)(2,1)S(1)}, u32[]{:S(2)}, u32[]{:S(2)}) collective-permute-start(bf16[1024,256]{1,0:T(8,128)(2,1)S(1)} %bitcast.56), channel_id=1, source_target_pairs={{0,8},{8,16},{16,24},{1,9},{9,17},{17,25},{2,10},{10,18},{18,26},{... | collective-permute-start | bytes 1572872 | tf_op jit(solution)/shard_map/ppermute | solution.py:129
  34.3 0.1 pad_dynamic-slice_fusion.1
  34.4 0.7 slice.32
  35.1 5.2 %collective-permute-start = (bf16[512,256]{1,0:T(8,128)(2,1)}, bf16[512,256]{1,0:T(8,128)(2,1)}, u32[]{:S(2)}, u32[]{:S(2)}) collective-permute-start(bf16[512,256]{1,0:T(8,128)(2,1)} %bitcast.11), channel_id=1, source_target_pairs={{0,16},{8,24},{1,17},{9,25},{2,18},{10,26},{3,19},{11,27},{4,20},{... | collective-permute-start | bytes 786440 | tf_op jit(solution)/shard_map/ppermute | solution.py:129
  40.3 0.1 pad_dynamic-slice_fusion
  40.4 1.4 %convert_reduce_fusion = s32[1024]{0:T(1024)S(1)} fusion(s32[1024]{0:T(1024)S(1)} %pad_dynamic-slice_fusion, s32[2560]{0:T(1024)S(1)} %pad_dynamic-slice_fusion.1), kind=kLoop, calls=%fused_computation | loop fusion | flops 7863296 | bytes 18432 | tf_op jit(solution)/shard_map/reduce_sum | solution.py:137
  41.8 0.0 copy-start.10
  41.8 0.6 slice.25.low_ref
  42.5 9.3 %collective-permute-done = bf16[512,256]{1,0:T(8,128)(2,1)} collective-permute-done((bf16[512,256]{1,0:T(8,128)(2,1)}, bf16[512,256]{1,0:T(8,128)(2,1)}, u32[]{:S(2)}, u32[]{:S(2)}) %collective-permute-start) | collective-permute-done | bytes 262176 | tf_op jit(solution)/shard_map/ppermute | solution.py:129
  51.8 0.0 collective-permute-done.1
  51.8 1.9 %pad_maximum_fusion.kv_ref = bf16[1536,256]{1,0:T(8,128)(2,1)} fusion(bf16[1024,256]{1,0:T(8,128)(2,1)S(1)} %collective-permute-done.1, bf16[512,256]{1,0:T(8,128)(2,1)} %collective-permute-done), kind=kLoop, calls=%fused_computation.6 | loop fusion | flops 1572864 | bytes 1572864 | tf_op jit(solution)/shard_map/concatenate | solution.py:132
  53.7 2.8 %all-to-all-done = bf16[8,128,1024]{2,1,0:T(8,128)(2,1)S(1)} async-done(((bf16[8,128,1024]{2,1,0:T(8,128)(2,1)}), bf16[8,128,1024]{2,1,0:T(8,128)(2,1)S(1)}, u32[]{:S(2)}, u32[]{:S(2)}) %all-to-all-start) | async-done | bytes 2097184 | tf_op jit(solution)/shard_map/all_to_all | solution.py:124
  56.4 1.3 copy-done.2
  57.8 3.8 %far_grads.1 = (f32[4,128,1024]{2,1,0:T(8,128)}, bf16[1536,256]{1,0:T(8,128)(2,1)}) custom-call(s32[4]{0:T(128)} %slice.25.low_ref, bf16[1024,1024]{1,0:T(8,128)(2,1)} %bitcast.53, f32[8,1024]{1,0:T(8,128)} %bitcast.65, s32[1,1024]{1,0:T(1,128)} %bitcast.67, bf16[1536,256]{1,0:T(8,128)(2,1)} %pad_maximum_fusion.kv_ref), custom_call_target="tpu_custom_call" | custom-call | flops 5368709120 | bytes 4194304 | tf_op jit(solution)/shard_map/far_grads/pallas_call | solution.py:144
  61.5 15.9 %near_grads.1 = (bf16[1024,512]{1,0:T(8,128)(2,1)}, f32[1024,256]{1,0:T(8,128)}) custom-call(s32[4]{0:T(128)} %slice.25.low_ref, bf16[1024,1024]{1,0:T(8,128)(2,1)} %bitcast.54, f32[8,1024]{1,0:T(8,128)} %bitcast.66, s32[1,1024]{1,0:T(1,128)} %bitcast.68, bf16[1024,256]{1,0:T(8,128)(2,1)} %bitcast.57, f32[4,128,1024]{2,1,0:T(8,128)} %get-tuple-element.7.dq_far), custom_call_target="tpu_custom_call" | custom-call | flops 2684354560 | bytes 4194304 | tf_op jit(solution)/shard_map/near_grads/pallas_call | solution.py:165
  77.4 3.7 %all-to-all-start.3 = ((bf16[8,128,512]{2,1,0:T(8,128)(2,1)}), bf16[8,128,512]{2,1,0:T(8,128)(2,1)S(1)}, u32[]{:S(2)}, u32[]{:S(2)}) async-start(bf16[8,128,512]{2,1,0:T(8,128)(2,1)} %bitcast.58), calls=%async_computation.3 | async-start | bytes 2097152 | tf_op jit(solution)/shard_map/all_to_all | solution.py:177
  81.2 1.3 collective-permute-start.2
  82.5 1.3 collective-permute-start.3
  83.8 36.8 %collective-permute-done.3 = bf16[512,256]{1,0:T(8,128)(2,1)S(1)} collective-permute-done((bf16[512,256]{1,0:T(8,128)(2,1)S(1)}, bf16[512,256]{1,0:T(8,128)(2,1)S(1)}, u32[]{:S(2)}, u32[]{:S(2)}) %collective-permute-start.3) | collective-permute-done | bytes 262176 | tf_op jit(solution)/shard_map/ppermute | solution.py:161
  120.6 0.0 collective-permute-done.2
  120.6 0.9 add_convert_fusion
  121.6 0.0 all-to-all-done.3
  121.6 3.8 %all-to-all-start.4 = ((bf16[8,128,256]{2,1,0:T(8,128)(2,1)}), bf16[8,128,256]{2,1,0:T(8,128)(2,1)S(1)}, u32[]{:S(2)}, u32[]{:S(2)}) async-start(bf16[8,128,256]{2,1,0:T(8,128)(2,1)} %bitcast.14), calls=%async_computation.4 | async-start | bytes 1048576 | tf_op jit(solution)/shard_map/all_to_all | solution.py:181
  125.4 1.1 copy.45
  126.5 7.8 %all-to-all-done.4 = bf16[8,128,256]{2,1,0:T(8,128)(2,1)S(1)} async-done(((bf16[8,128,256]{2,1,0:T(8,128)(2,1)}), bf16[8,128,256]{2,1,0:T(8,128)(2,1)S(1)}, u32[]{:S(2)}, u32[]{:S(2)}) %all-to-all-start.4) | async-done | bytes 524320 | tf_op jit(solution)/shard_map/all_to_all | solution.py:181
  134.3 0.1 slice_bitcast_fusion
  134.4 0.8 copy.55
  135.2 0.8 copy.56
  (17 shorter events, 0.1 us)
Async XLA Ops:
  0.6 9.5 %copy-start = (bf16[128,1024]{1,0:T(8,128)(2,1)S(1)}, bf16[128,1024]{1,0:T(8,128)(2,1)}, u32[]{:S(2)}) copy-start(bf16[128,1024]{1,0:T(8,128)(2,1)} %param.8) | copy-start | bytes 786436
  3.6 6.6 %copy-start.7 = (bf16[128,1024]{1,0:T(8,128)(2,1)S(1)}, bf16[128,1024]{1,0:T(8,128)(2,1)}, u32[]{:S(2)}) copy-start(bf16[128,1024]{1,0:T(8,128)(2,1)} %param.9) | copy-start | bytes 786436
  4.2 14.2 %copy-start.1 = (bf16[128,4096]{1,0:T(8,128)(2,1)S(1)}, bf16[128,4096]{1,0:T(8,128)(2,1)}, u32[]{:S(2)}) copy-start(bf16[128,4096]{1,0:T(8,128)(2,1)} %param.11) | copy-start | bytes 3145732
  4.2 14.2 %copy-start.5 = (bf16[128,4096]{1,0:T(8,128)(2,1)S(1)}, bf16[128,4096]{1,0:T(8,128)(2,1)}, u32[]{:S(2)}) copy-start(bf16[128,4096]{1,0:T(8,128)(2,1)} %param.7) | copy-start | bytes 3145732
  4.9 10.0 %all-to-all-start.1 = ((f32[8,8,128]{2,1,0:T(8,128)}), f32[8,8,128]{2,1,0:T(8,128)S(1)}, u32[]{:S(2)}, u32[]{:S(2)}) async-start(f32[8,8,128]{2,1,0:T(8,128)} %maximum_bitcast_fusion.2), calls=%async_computation.1 | async-start | bytes 65536 | tf_op jit(solution)/shard_map/all_to_all | solution.py:120
  14.9 3.7 %copy-start.9 = (f32[8,8,128]{2,1,0:T(8,128)}, f32[8,8,128]{2,1,0:T(8,128)S(1)}, u32[]{:S(2)}) copy-start(f32[8,8,128]{2,1,0:T(8,128)S(1)} %all-to-all-done.1) | copy-start | bytes 98308
  14.9 12.3 %all-to-all-start.2 = ((bf16[8,128,256]{2,1,0:T(8,128)(2,1)}), bf16[8,128,256]{2,1,0:T(8,128)(2,1)S(1)}, u32[]{:S(2)}, u32[]{:S(2)}) async-start(bf16[8,128,256]{2,1,0:T(8,128)(2,1)} %maximum_bitcast_fusion.1), calls=%async_computation.2 | async-start | bytes 1048576 | tf_op jit(solution)/shard_map/all_to_all | solution.py:113
  20.2 14.1 %copy-start.8 = (s32[4096]{0:T(1024)S(1)}, s32[4096]{0:T(1024)}, u32[]{:S(2)}) copy-start(s32[4096]{0:T(1024)} %param.13) | copy-start | bytes 49156
  27.2 7.2 %copy-start.3 = (bf16[8,128,256]{2,1,0:T(8,128)(2,1)}, bf16[8,128,256]{2,1,0:T(8,128)(2,1)S(1)}, u32[]{:S(2)}) copy-start(bf16[8,128,256]{2,1,0:T(8,128)(2,1)S(1)} %all-to-all-done.2) | copy-start | bytes 1572868
  27.2 29.2 %all-to-all-start = ((bf16[8,128,1024]{2,1,0:T(8,128)(2,1)}), bf16[8,128,1024]{2,1,0:T(8,128)(2,1)S(1)}, u32[]{:S(2)}, u32[]{:S(2)}) async-start(bf16[8,128,1024]{2,1,0:T(8,128)(2,1)} %maximum_bitcast_fusion), calls=%async_computation | async-start | bytes 4194304 | tf_op jit(solution)/shard_map/all_to_all | solution.py:124
  30.8 21.0 %collective-permute-start.1 = (bf16[1024,256]{1,0:T(8,128)(2,1)S(1)}, bf16[1024,256]{1,0:T(8,128)(2,1)S(1)}, u32[]{:S(2)}, u32[]{:S(2)}) collective-permute-start(bf16[1024,256]{1,0:T(8,128)(2,1)S(1)} %bitcast.56), channel_id=1, source_target_pairs={{0,8},{8,16},{16,24},{1,9},{9,17},{17,25},{2,10},{10,18},{18,26},{... | collective-permute-start | bytes 1572872 | tf_op jit(solution)/shard_map/ppermute | solution.py:129
  35.1 16.6 %collective-permute-start = (bf16[512,256]{1,0:T(8,128)(2,1)}, bf16[512,256]{1,0:T(8,128)(2,1)}, u32[]{:S(2)}, u32[]{:S(2)}) collective-permute-start(bf16[512,256]{1,0:T(8,128)(2,1)} %bitcast.11), channel_id=1, source_target_pairs={{0,16},{8,24},{1,17},{9,25},{2,18},{10,26},{3,19},{11,27},{4,20},{... | collective-permute-start | bytes 786440 | tf_op jit(solution)/shard_map/ppermute | solution.py:129
  41.8 14.6 %copy-start.10 = (s32[1024]{0:T(1024)}, s32[1024]{0:T(1024)S(1)}, u32[]{:S(2)}) copy-start(s32[1024]{0:T(1024)S(1)} %convert_reduce_fusion) | copy-start | bytes 12292
  56.4 1.3 copy-start.2
  77.4 3.7 %copy-start.6 = (bf16[1536,256]{1,0:T(8,128)(2,1)S(1)}, bf16[1536,256]{1,0:T(8,128)(2,1)}, u32[]{:S(2)}) copy-start(bf16[1536,256]{1,0:T(8,128)(2,1)} %get-tuple-element.10) | copy-start | bytes 2359300
  77.4 43.2 %copy-start.4 = (f32[1024,256]{1,0:T(8,128)S(1)}, f32[1024,256]{1,0:T(8,128)}, u32[]{:S(2)}) copy-start(f32[1024,256]{1,0:T(8,128)} %get-tuple-element.9) | copy-start | bytes 3145732
  77.4 44.2 %all-to-all-start.3 = ((bf16[8,128,512]{2,1,0:T(8,128)(2,1)}), bf16[8,128,512]{2,1,0:T(8,128)(2,1)S(1)}, u32[]{:S(2)}, u32[]{:S(2)}) async-start(bf16[8,128,512]{2,1,0:T(8,128)(2,1)} %bitcast.58), calls=%async_computation.3 | async-start | bytes 2097152 | tf_op jit(solution)/shard_map/all_to_all | solution.py:177
  81.2 39.4 %collective-permute-start.2 = (bf16[1024,256]{1,0:T(8,128)(2,1)S(1)}, bf16[1024,256]{1,0:T(8,128)(2,1)S(1)}, u32[]{:S(2)}, u32[]{:S(2)}) collective-permute-start(bf16[1024,256]{1,0:T(8,128)(2,1)S(1)} %slice.28), channel_id=1, source_target_pairs={{8,0},{16,8},{24,16},{9,1},{17,9},{25,17},{10,2},{18,10},{26,18},{... | collective-permute-start | bytes 1572872 | tf_op jit(solution)/shard_map/ppermute | solution.py:161
  82.5 38.1 %collective-permute-start.3 = (bf16[512,256]{1,0:T(8,128)(2,1)S(1)}, bf16[512,256]{1,0:T(8,128)(2,1)S(1)}, u32[]{:S(2)}, u32[]{:S(2)}) collective-permute-start(bf16[512,256]{1,0:T(8,128)(2,1)S(1)} %slice.29), channel_id=1, source_target_pairs={{16,0},{24,8},{17,1},{25,9},{18,2},{26,10},{19,3},{27,11},{20,4},{... | collective-permute-start | bytes 786440 | tf_op jit(solution)/shard_map/ppermute | solution.py:161
  121.6 12.7 %all-to-all-start.4 = ((bf16[8,128,256]{2,1,0:T(8,128)(2,1)}), bf16[8,128,256]{2,1,0:T(8,128)(2,1)S(1)}, u32[]{:S(2)}, u32[]{:S(2)}) async-start(bf16[8,128,256]{2,1,0:T(8,128)(2,1)} %bitcast.14), calls=%async_computation.4 | async-start | bytes 1048576 | tf_op jit(solution)/shard_map/all_to_all | solution.py:181
where the time goes:
time: 135 us; the launch traced here: 136 us
  waiting for transfers between devices  67.4 us (50%)
  starting transfers between devices  31.1 us (23%)
  Pallas kernels  19.7 us (15%)
  other arithmetic  10.5 us (8%)
  local copies, waits for them, and re-layouts  6.43 us (5%)
    ppermute x2, waiting for transfers between devices, shards(): lax.ppermute(dkv_far[at:at + sizes[by - 1]], 'outer', [(i + by, i) for i...  36.8 us
    pallas_call x1, Pallas kernels, shards(): pl.pallas_call(functools.partial(near_kernel, window), out_shape=(jax.Sha...  15.9 us
    ppermute x2, waiting for transfers between devices, shards(): lax.ppermute(kv[rows - sizes[by - 1]:], 'outer', [(i, i + by) for i in ra...  9.33 us
    ppermute x2, starting transfers between devices, shards(): lax.ppermute(kv[rows - sizes[by - 1]:], 'outer', [(i, i + by) for i in ra...  8.68 us
    all_to_all x1, waiting for transfers between devices, shards(): lax.all_to_all(dkv.astype(jnp.bfloat16).reshape(parts, tokens, 2 * d), GR...  7.77 us
    all_to_all x1, waiting for transfers between devices, shards(): kv = lax.all_to_all(kv, GROUP, 0, 0).reshape(rows, 2 * d)  6.94 us
    all_to_all x1, starting transfers between devices, shards(): lax.all_to_all(stat, GROUP, 0, 0).transpose(1, 0, 2)  5.2 us
    all_to_all x1, starting transfers between devices, shards(): lax.all_to_all(dkv.astype(jnp.bfloat16).reshape(parts, tokens, 2 * d), GR...  3.85 us
  transfers between devices with their start and end apart: 9, of which 6 were waited for; matrix products, arithmetic and copies ran while one was open for 7% of the time, Pallas kernels for 0%

commit v1 on v0

v1 whole, which is shorter than its diff:
```python
import functools
import math

import jax
import jax.numpy as jnp
from jax import lax
from jax.experimental import pallas as pl
from jax.experimental.pallas import tpu as pltpu
from jax.sharding import Mesh, PartitionSpec as P


HEAD_SIZE = 128
LONGEST = 1536
TILE_Q = 256
TILE_K = 256
LOG2E = math.log2(math.e)
GROUP = ("inner", "head")


def dot(a, b, dims):
    return lax.dot_general(a, b, (dims, ((), ())), preferred_element_type=jnp.float32)


def tile_grads(get, stat_ref, start_ref, kv_ref, dq_t, dkv, q0, k0, key_pos, query_pos):
    d = HEAD_SIZE
    factor = LOG2E / math.sqrt(d)
    heads = len(get)
    rows = pl.ds(q0, TILE_Q)
    keys = pl.ds(k0, TILE_K)
    k = kv_ref[keys, :d]
    v = kv_ref[keys, d:]
    k_t = k.T
    at = key_pos + lax.broadcasted_iota(jnp.int32, (TILE_K, TILE_Q), 0)
    last = query_pos + lax.broadcasted_iota(jnp.int32, (1, TILE_Q), 1)
    allowed = (at >= start_ref[:, rows]) & (at <= last)
    grad_k = jnp.zeros((TILE_K, d), jnp.float32)
    grad_v = jnp.zeros((TILE_K, d), jnp.float32)
    for h in range(heads):
        q, e = get[h](q0)
        scores = dot(k, q, ((1,), (1,)))
        dprobs = dot(v, e, ((1,), (1,)))
        raised = jnp.where(allowed, scores * factor - stat_ref[2 * h : 2 * h + 1, rows], -jnp.inf)
        probs = jnp.exp2(raised)
        ds = (probs * (dprobs - stat_ref[2 * h + 1 : 2 * h + 2, rows])).astype(jnp.bfloat16)
        grad_v += dot(probs.astype(jnp.bfloat16), e, ((1,), (0,)))
        grad_k += dot(ds, q, ((1,), (0,)))
        dq_t[h, :, rows] += dot(k_t, ds, ((1,), (0,)))
    dkv[keys, :d] += grad_k
    dkv[keys, d:] += grad_v


def getters(bulk_refs, tokens):
    d = HEAD_SIZE
    get = []
    for ref in bulk_refs:
        heads = ref.shape[2] // (2 * d)
        for h in range(heads):

            def one(q0, ref=ref, h=h, heads=heads):
                chunks = pl.ds(q0 // tokens, TILE_Q // tokens)
                return tuple(
                    ref[chunks, :tokens, (n * heads + h) * d : (n * heads + h + 1) * d].reshape(TILE_Q, d)
                    for n in range(2)
                )

            get.append(one)
    return get


def sweep(get, low_ref, stat_ref, start_ref, kv_ref, dq_t, dkv, base, window, finish):
    rows = dq_t.shape[2]
    keys = kv_ref.shape[0]

    def per_query(t, _):
        q0 = pl.multiple_of(t * TILE_Q, TILE_Q)

        def per_key(j, _):
            k0 = pl.multiple_of(j * TILE_K, TILE_K)
            tile_grads(get, stat_ref, start_ref, kv_ref, dq_t, dkv, q0, k0, base + k0, window + q0)
            return 0

        first = jnp.clip(low_ref[t] - base, 0, keys) // TILE_K
        end = jnp.minimum(window + q0 + TILE_Q - base, keys) // TILE_K
        lax.fori_loop(first, end, per_key, 0)
        finish(q0)
        return 0

    lax.fori_loop(0, rows // TILE_Q, per_query, 0)


def write_dq(dq_t, heads, dq_out, q0):
    d = HEAD_SIZE
    scale = 1.0 / math.sqrt(d)
    for n, h in enumerate(heads):
        done = dq_t[h, :, pl.ds(q0, TILE_Q)] * scale
        dq_out[pl.ds(q0, TILE_Q), n * d : (n + 1) * d] = done.T.astype(dq_out.dtype)


def early_kernel(tokens, window, low_ref, bulk_a, stat_ref, start_ref, kv_ref, dq_t, dkv):
    dq_t[...] = jnp.zeros_like(dq_t)
    dkv[...] = jnp.zeros_like(dkv)
    get = getters([bulk_a], tokens)
    sweep(get, low_ref, stat_ref, start_ref, kv_ref, dq_t, dkv, window, window, lambda q0: None)


def far_kernel(
    tokens, low_ref, bulk_a, bulk_b, stat_ref, start_ref, kv_ref, dq_near, dq_out, dq_rest, dkv_out, dq_t, dkv
):
    d = HEAD_SIZE
    half = dq_near.shape[0]
    heads = dq_t.shape[0]
    dq_t[:half] = dq_near[...]
    dq_t[half:] = jnp.zeros_like(dq_rest)
    dkv[...] = jnp.zeros_like(dkv)
    get = getters([bulk_a, bulk_b], tokens)

    def finish(q0):
        write_dq(dq_t, range(half), dq_out, q0)

    sweep(get, low_ref, stat_ref, start_ref, kv_ref, dq_t, dkv, 0, kv_ref.shape[0], finish)
    dq_rest[...] = dq_t[half:heads]
    dkv_out[:, :d] = (dkv[:, :d] * (1.0 / math.sqrt(d))).astype(dkv_out.dtype)
    dkv_out[:, d:] = dkv[:, d:].astype(dkv_out.dtype)


def late_kernel(
    tokens, window, low_ref, bulk_b, stat_ref, start_ref, kv_ref, dq_far, dkv_near, dq_out, dkv, dq_t
):
    dq_t[...] = dq_far[...]
    dkv[...] = dkv_near[...]
    get = getters([bulk_b], tokens)

    def finish(q0):
        write_dq(dq_t, range(dq_t.shape[0]), dq_out, q0)

    sweep(get, low_ref, stat_ref, start_ref, kv_ref, dq_t, dkv, window, window, finish)
    dkv[:, :HEAD_SIZE] = dkv[:, :HEAD_SIZE] * (1.0 / math.sqrt(HEAD_SIZE))


def pieces_of(x):
    first = lax.reduce_precision(x, 8, 7)
    second = lax.reduce_precision(x - first, 8, 7)
    return [first, second, x - first - second]


def packed(query, grad, stat, parts):
    _, _, wide = query.shape
    both = jnp.concatenate([query, grad], axis=2).transpose(1, 0, 2)
    tail = jnp.stack(pieces_of(stat), axis=1).reshape(parts, -1, 2 * wide).astype(jnp.bfloat16)
    pad = -tail.shape[1] % 8
    return jnp.concatenate([both, jnp.pad(tail, ((0, 0), (0, pad), (0, 0)))], axis=1)


def unpacked_stat(bulk, tokens, lines):
    parts, _, wide = bulk.shape
    used = 3 * lines * tokens // wide
    tail = bulk[:, tokens : tokens + used].astype(jnp.float32).reshape(parts, 3, lines, tokens)
    stat = tail[:, 0] + tail[:, 1] + tail[:, 2]
    return stat.transpose(1, 0, 2).reshape(lines, parts * tokens)


def whole(query, key, value, out, output_gradient, log_sum_exp, segment_ids):
    d = HEAD_SIZE
    tokens = query.shape[0]
    parts = lax.axis_size(GROUP)
    outers = lax.axis_size("outer")
    rows = tokens * parts
    heads = query.shape[1] // key.shape[1]
    half = heads // 2
    window = LONGEST
    place = lax.axis_index("outer")

    kv = jnp.concatenate(
        [key.reshape(tokens, parts, d), value.reshape(tokens, parts, d)], axis=2
    ).transpose(1, 0, 2)
    kv = lax.all_to_all(kv, GROUP, 0, 0).reshape(rows, 2 * d)
    delta = jnp.sum(
        (output_gradient.astype(jnp.float32) * out.astype(jnp.float32)).reshape(tokens, -1, d), axis=2
    )
    stat = jnp.stack([log_sum_exp * LOG2E, delta], axis=2).reshape(tokens, parts, 2 * heads).transpose(1, 2, 0)
    query_heads = query.reshape(tokens, parts, heads * d)
    grad_heads = output_gradient.reshape(tokens, parts, heads * d)
    bulk = []
    for n in range(2):
        cut = slice(n * half * d, (n + 1) * half * d)
        sent = packed(
            query_heads[:, :, cut], grad_heads[:, :, cut], stat[:, 2 * half * n : 2 * half * (n + 1)], parts
        )
        bulk.append(lax.all_to_all(sent, GROUP, 0, 0))
    stats = [unpacked_stat(b, tokens, 2 * half) for b in bulk]

    steps = -(-window // rows)
    sizes = [min(rows, window - by * rows) for by in range(steps)]
    arrived = []
    for by in range(1, steps + 1):
        arrived.append(
            lax.ppermute(kv[rows - sizes[by - 1] :], "outer", [(i, i + by) for i in range(outers - by)])
        )
    kv_far = jnp.concatenate(arrived[::-1], axis=0)

    padded = jnp.concatenate([jnp.full((window,), -1, segment_ids.dtype), segment_ids])
    seg_keys = lax.dynamic_slice_in_dim(padded, place * rows, window + rows, 0)
    seg_query = seg_keys[window:]
    start = jnp.sum((seg_keys[:, None] < seg_query[None, :]).astype(jnp.int32), axis=0)
    low = start[::TILE_Q]
    start = start[None, :]

    smem = pl.BlockSpec(memory_space=pltpu.SMEM)
    vmem = pl.BlockSpec(memory_space=pltpu.VMEM)
    flops = 10 * rows * d * half * 512
    dq_shape = jax.ShapeDtypeStruct((half, d, rows), jnp.float32)
    dq_done = jax.ShapeDtypeStruct((rows, half * d), jnp.bfloat16)
    dkv_shape = jax.ShapeDtypeStruct((rows, 2 * d), jnp.float32)

    def call(kernel, out_shape, scratch, work, *operands):
        return pl.pallas_call(
            kernel,
            out_shape=out_shape,
            in_specs=[smem] + [vmem] * (len(operands) - 1),
            out_specs=(vmem,) * len(out_shape),
            scratch_shapes=scratch,
            cost_estimate=pl.CostEstimate(flops=work, bytes_accessed=1 << 22, transcendentals=0),
        )(*operands)

    dq_near, dkv_near = call(
        functools.partial(early_kernel, tokens, window),
        (dq_shape, dkv_shape),
        [],
        flops,
        *(low, bulk[0], stats[0], start, kv),
    )
    dq_a, dq_far, dkv_far = call(
        functools.partial(far_kernel, tokens),
        (dq_done, dq_shape, jax.ShapeDtypeStruct((window, 2 * d), jnp.bfloat16)),
        [pltpu.VMEM((heads, d, rows), jnp.float32), pltpu.VMEM((window, 2 * d), jnp.float32)],
        4 * flops,
        *(low, bulk[0], bulk[1], jnp.concatenate(stats, axis=0), start, kv_far, dq_near),
    )
    returned = []
    at = window
    for by in range(1, steps + 1):
        at -= sizes[by - 1]
        returned.append(
            lax.ppermute(
                dkv_far[at : at + sizes[by - 1]], "outer", [(i + by, i) for i in range(outers - by)]
            )
        )
    dq_a = lax.all_to_all(dq_a.reshape(parts, tokens, half * d), GROUP, 0, 0)
    dq_b, dkv = call(
        functools.partial(late_kernel, tokens, window),
        (dq_done, dkv_shape),
        [pltpu.VMEM((half, d, rows), jnp.float32)],
        flops,
        *(low, bulk[1], stats[1], start, kv, dq_far, dkv_near),
    )
    dq_b = lax.all_to_all(dq_b.reshape(parts, tokens, half * d), GROUP, 0, 0)
    for by in range(1, steps + 1):
        part = returned[by - 1].astype(jnp.float32)
        dkv = dkv + jnp.pad(part, ((rows - sizes[by - 1], 0), (0, 0)))
    dkv = lax.all_to_all(dkv.astype(jnp.bfloat16).reshape(parts, tokens, 2 * d), GROUP, 0, 0)
    dkv = dkv.transpose(1, 0, 2)
    return (
        jnp.concatenate([dq_a, dq_b], axis=2).transpose(1, 0, 2).reshape(tokens, -1),
        dkv[:, :, :d].reshape(tokens, -1),
        dkv[:, :, d:].reshape(tokens, -1),
    )


def solution(mesh):
    head = mesh.shape["head"]
    seq = mesh.shape["seq"]

    def run(query, key, value, out, output_gradient, log_sum_exp, segment_ids):
        inner = key.shape[1] // HEAD_SIZE // head
        finer = Mesh(mesh.devices.reshape(seq // inner, inner, head), ("outer", "inner", "head"))
        rows = P(("outer", "inner", "head"), None)
        return jax.shard_map(
            whole,
            mesh=finer,
            in_specs=(rows,) * 6 + (P(),),
            out_specs=(rows,) * 3,
            check_vma=False,
        )(query, key, value, out, output_gradient, log_sum_exp, segment_ids)

    return run
```

time: 135 us -> 149 us (1.10); the launches traced: 136 us -> 148 us
  local copies, waits for them, and re-layouts: 6.43 us -> 14.9 us
  waiting for transfers between devices: 67.4 us -> 61.6 us
  starting transfers between devices: 31.1 us -> 35.7 us
  Pallas kernels: 19.7 us -> 24.1 us
    ppermute x4, waiting for transfers between devices: 46.1 us -> 32.3 us  [the longest x2 32.3 us: whole(): lax.ppermute(dkv_far[at:at + sizes[by - 1]], 'outer', [(i + by, i) for i...]
    all_to_all x5 -> x6, waiting for transfers between devices: 21.2 us -> 29.3 us  [the longest x2 16.3 us: whole(): bulk.append(lax.all_to_all(sent, GROUP, 0, 0))]
    unnamed x24 -> x35, local copies, waits for them, and re-layouts: 1.88 us -> 6.59 us
    pallas_call x2 -> x3, Pallas kernels: 19.7 us -> 24.1 us  [call(): pl.pallas_call(kernel, out_shape=out_shape, in_specs=[smem] + [vmem] * (l...]
    all_to_all x5 -> x6, starting transfers between devices: 19.8 us -> 24.1 us  [the longest x2 7.76 us: whole(): bulk.append(lax.all_to_all(sent, GROUP, 0, 0))]
    slice x5 -> x7, local copies, waits for them, and re-layouts: 1.47 us -> 4.28 us  [the longest x1 0.97 us: whole(): kv[rows - sizes[by - 1]:]]
    concatenate x1 -> x4, other arithmetic: 1.88 us -> 4.68 us  [the longest x2 2.16 us: packed(): jnp.concatenate([both, jnp.pad(tail, ((0, 0), (0, pad), (0, 0)))], axis=1)]
    transpose x3, other arithmetic: 3.11 us -> 1.01 us  [the longest x1 0.85 us: whole(): kv = jnp.concatenate([key.reshape(tokens, parts, d), value.reshape(tokens...]
  transfers between devices with their start and end apart: 9 -> 10, of which waited for: 6 -> 5; matrix products, arithmetic and copies ran while one was open for 7% -> 12% of each run, Pallas kernels for 0% -> 6%
where the time goes in v1:
time: 149 us; the launch traced here: 148 us
  waiting for transfers between devices  61.6 us (41%)
  starting transfers between devices  35.7 us (24%)
  Pallas kernels  24.1 us (16%)
  local copies, waits for them, and re-layouts  14.9 us (10%)
  other arithmetic  10.3 us (7%)
    ppermute x2, waiting for transfers between devices, whole(): lax.ppermute(dkv_far[at:at + sizes[by - 1]], 'outer', [(i + by, i) for i...  32.3 us
    pallas_call x3, Pallas kernels, call(): pl.pallas_call(kernel, out_shape=out_shape, in_specs=[smem] + [vmem] * (l...  24.1 us
    all_to_all x2, waiting for transfers between devices, whole(): bulk.append(lax.all_to_all(sent, GROUP, 0, 0))  16.3 us
    ppermute x2, starting transfers between devices, whole(): lax.ppermute(kv[rows - sizes[by - 1]:], 'outer', [(i, i + by) for i in ra...  9.02 us
    all_to_all x2, starting transfers between devices, whole(): bulk.append(lax.all_to_all(sent, GROUP, 0, 0))  7.76 us
    all_to_all x1, waiting for transfers between devices, whole(): lax.all_to_all(dkv.astype(jnp.bfloat16).reshape(parts, tokens, 2 * d), GR...  7.69 us
    unnamed x35, local copies, waits for them, and re-layouts  6.59 us
    all_to_all x1, waiting for transfers between devices, whole(): dq_b = lax.all_to_all(dq_b.reshape(parts, tokens, half * d), GROUP, 0, 0)  5.39 us
  transfers between devices with their start and end apart: 10, of which 5 were waited for; matrix products, arithmetic and copies ran while one was open for 12% of the time, Pallas kernels for 6%

profile of v1, /device:TPU:0, one launch (start us, length us, event | category | flops | bytes accessed | tf_op | source)
XLA Modules:
  0.0 147.7 jit_solution(14026411830080338371)
XLA Ops:
  0.7 0.9 copy-done
  1.6 1.1 copy_bitcast_fusion.2
  2.7 0.9 maximum_bitcast_fusion.3
  3.5 5.2 %all-to-all-start.2 = ((bf16[8,128,256]{2,1,0:T(8,128)(2,1)}), bf16[8,128,256]{2,1,0:T(8,128)(2,1)}, u32[]{:S(2)}, u32[]{:S(2)}) async-start(bf16[8,128,256]{2,1,0:T(8,128)(2,1)} %maximum_bitcast_fusion.3), calls=%async_computation.2 | async-start | bytes 1048576 | tf_op jit(solution)/shard_map/all_to_all | solution.py:176
  8.7 0.1 copy.108
  8.9 0.7 copy.104
  9.5 0.9 fusion.18
  10.4 0.7 copy.106
  11.1 0.9 fusion.19
  12.0 0.5 copy-done.6
  12.5 0.2 multiply_bitcast_fusion
  12.8 0.4 copy.142
  13.1 0.6 reduce_sum.19
  13.9 1.2 copy.129
  15.1 1.2 copy.130
  16.6 1.1 pad_maximum_fusion.1
  17.7 4.2 %all-to-all-start.1 = ((bf16[8,136,512]{2,1,0:T(8,128)(2,1)}), bf16[8,136,512]{2,1,0:T(8,128)(2,1)S(1)}, u32[]{:S(2)}, u32[]{:S(2)}) async-start(bf16[8,136,512]{2,1,0:T(8,128)(2,1)} %pad_maximum_fusion.1), calls=%async_computation.1 | async-start | bytes 2228224 | tf_op jit(solution)/shard_map/all_to_all | solution.py:189
  21.9 0.2 copy.127
  22.1 0.2 copy.128
  22.6 1.1 pad_maximum_fusion
  23.6 13.4 %all-to-all-done.1.bulk_b = bf16[8,136,512]{2,1,0:T(8,128)(2,1)S(1)} async-done(((bf16[8,136,512]{2,1,0:T(8,128)(2,1)}), bf16[8,136,512]{2,1,0:T(8,128)(2,1)S(1)}, u32[]{:S(2)}, u32[]{:S(2)}) %all-to-all-start.1) | async-done | bytes 1114144 | tf_op jit(solution)/shard_map/all_to_all | solution.py:189
  37.1 3.6 %all-to-all-start = ((bf16[8,136,512]{2,1,0:T(8,128)(2,1)}), bf16[8,136,512]{2,1,0:T(8,128)(2,1)S(1)}, u32[]{:S(2)}, u32[]{:S(2)}) async-start(bf16[8,136,512]{2,1,0:T(8,128)(2,1)} %pad_maximum_fusion), calls=%async_computation | async-start | bytes 2228224 | tf_op jit(solution)/shard_map/all_to_all | solution.py:189
  40.8 1.4 convert_reduce_fusion
  42.3 0.6 slice.67.low_ref
  42.9 1.0 slice.102
  43.8 5.5 %collective-permute-start = (bf16[512,256]{1,0:T(8,128)(2,1)S(1)}, bf16[512,256]{1,0:T(8,128)(2,1)}, u32[]{:S(2)}, u32[]{:S(2)}) collective-permute-start(bf16[512,256]{1,0:T(8,128)(2,1)S(1)} %bitcast.99), channel_id=1, source_target_pairs={{0,16},{8,24},{1,17},{9,25},{2,18},{10,26},{3,19},{11,27},{4,20},{... | collective-permute-start | bytes 786440 | tf_op jit(solution)/shard_map/ppermute | solution.py:197
  49.3 3.5 %collective-permute-start.1 = (bf16[1024,256]{1,0:T(8,128)(2,1)}, bf16[1024,256]{1,0:T(8,128)(2,1)S(1)}, u32[]{:S(2)}, u32[]{:S(2)}) collective-permute-start(bf16[1024,256]{1,0:T(8,128)(2,1)} %bitcast.18.kv_ref), channel_id=1, source_target_pairs={{0,8},{8,16},{16,24},{1,9},{9,17},{17,25},{2,10},{10,18},{18,26},{... | collective-permute-start | bytes 1572872 | tf_op jit(solution)/shard_map/ppermute | solution.py:197
  52.9 2.8 %all-to-all-done.bulk_a = bf16[8,136,512]{2,1,0:T(8,128)(2,1)S(1)} async-done(((bf16[8,136,512]{2,1,0:T(8,128)(2,1)}), bf16[8,136,512]{2,1,0:T(8,128)(2,1)S(1)}, u32[]{:S(2)}, u32[]{:S(2)}) %all-to-all-start) | async-done | bytes 1114144 | tf_op jit(solution)/shard_map/all_to_all | solution.py:189
  55.9 0.6 pad_maximum_fusion.4.stat_ref
  56.5 0.3 copy-done.3
  56.8 9.5 %shard_map.94 = (f32[2,128,1024]{2,1,0:T(8,128)}, f32[1024,256]{1,0:T(8,128)}) custom-call(s32[4]{0:T(128)} %slice.67.low_ref, bf16[8,136,512]{2,1,0:T(8,128)(2,1)} %copy-done.3, f32[4,1024]{1,0:T(4,128)} %copy-done.10, s32[1,1024]{1,0:T(1,128)} %bitcast.104, bf16[1024,256]{1,0:T(8,128)(2,1)} %bitcast.18.kv_ref), custom_call_target="tpu_custom_call" | custom-call | flops 1342177280 | bytes 4194304 | tf_op jit(solution)/shard_map/pallas_call | solution.py:216
  66.2 1.9 %pad_maximum_fusion.2.kv_ref = bf16[1536,256]{1,0:T(8,128)(2,1)} fusion(bf16[1024,256]{1,0:T(8,128)(2,1)S(1)} %collective-permute-done.1, bf16[512,256]{1,0:T(8,128)(2,1)} %collective-permute-done), kind=kLoop, calls=%fused_computation.8 | loop fusion | flops 1572864 | bytes 1572864 | tf_op jit(solution)/shard_map/concatenate | solution.py:199
  68.1 4.3 %shard_map.95 = (bf16[1024,256]{1,0:T(8,128)(2,1)}, f32[2,128,1024]{2,1,0:T(8,128)}, bf16[1536,256]{1,0:T(8,128)(2,1)}) custom-call(s32[4]{0:T(128)} %slice.67.low_ref, bf16[8,136,512]{2,1,0:T(8,128)(2,1)} %copy-done.3, bf16[8,136,512]{2,1,0:T(8,128)(2,1)} %copy-done.2, f32[8,1024]{1,0:T(8,128)} %pad_maximum_fusion.4.stat_ref, s32[1,1024]{1,0:T(1,128)} %bitcast.105, ...), custom_call_target="tpu_custom_call" | custom-call | flops 5368709120 | bytes 4194304 | tf_op jit(solution)/shard_map/pallas_call | solution.py:216
  72.4 10.4 %shard_map.96 = (bf16[1024,256]{1,0:T(8,128)(2,1)}, f32[1024,256]{1,0:T(8,128)}) custom-call(s32[4]{0:T(128)} %slice.67.low_ref, bf16[8,136,512]{2,1,0:T(8,128)(2,1)} %copy-done.2, f32[4,1024]{1,0:T(4,128)} %copy-done.9, s32[1,1024]{1,0:T(1,128)} %bitcast.106, bf16[1024,256]{1,0:T(8,128)(2,1)} %bitcast.18.kv_ref, f32[2,128,1024]{2,1,0:T(8,128)} %get-tuple-element.12.dq_far, ...), custom_call_target="tpu_custom_call" | custom-call | flops 1342177280 | bytes 4194304 | tf_op jit(solution)/shard_map/pallas_call | solution.py:216
  82.8 3.9 %all-to-all-start.4 = ((bf16[8,128,256]{2,1,0:T(8,128)(2,1)}), bf16[8,128,256]{2,1,0:T(8,128)(2,1)S(1)}, u32[]{:S(2)}, u32[]{:S(2)}) async-start(bf16[8,128,256]{2,1,0:T(8,128)(2,1)} %bitcast.98), calls=%async_computation.4 | async-start | bytes 1048576 | tf_op jit(solution)/shard_map/all_to_all | solution.py:256
  86.7 0.8 slice.84
  87.6 1.3 collective-permute-start.2
  88.9 1.3 collective-permute-start.3
  90.2 5.4 %all-to-all-done.4 = bf16[8,128,256]{2,1,0:T(8,128)(2,1)S(1)} async-done(((bf16[8,128,256]{2,1,0:T(8,128)(2,1)}), bf16[8,128,256]{2,1,0:T(8,128)(2,1)S(1)}, u32[]{:S(2)}, u32[]{:S(2)}) %all-to-all-start.4) | async-done | bytes 524320 | tf_op jit(solution)/shard_map/all_to_all | solution.py:256
  95.6 3.5 %all-to-all-start.3 = ((bf16[8,128,256]{2,1,0:T(8,128)(2,1)}), bf16[8,128,256]{2,1,0:T(8,128)(2,1)S(1)}, u32[]{:S(2)}, u32[]{:S(2)}) async-start(bf16[8,128,256]{2,1,0:T(8,128)(2,1)} %bitcast.97), calls=%async_computation.3 | async-start | bytes 1048576 | tf_op jit(solution)/shard_map/all_to_all | solution.py:248
  99.1 32.3 %collective-permute-done.3 = bf16[512,256]{1,0:T(8,128)(2,1)S(1)} collective-permute-done((bf16[512,256]{1,0:T(8,128)(2,1)S(1)}, bf16[512,256]{1,0:T(8,128)(2,1)S(1)}, u32[]{:S(2)}, u32[]{:S(2)}) %collective-permute-start.3) | collective-permute-done | bytes 262176 | tf_op jit(solution)/shard_map/ppermute | solution.py:244
  131.3 2.0 %add_convert_fusion = bf16[1024,256]{1,0:T(8,128)(2,1)} fusion(f32[1024,256]{1,0:T(8,128)S(1)} %copy-done.5, bf16[1024,256]{1,0:T(8,128)(2,1)} %collective-permute-done.2, bf16[512,256]{1,0:T(8,128)(2,1)S(1)} %collective-permute-done.3), kind=kLoop, calls=%fused_computation.7 | loop fusion | flops 1310720 | bytes 2359296 | tf_op jit(solution)/shard_map/convert_element_type | solution.py:260
  133.3 3.8 %all-to-all-start.5 = ((bf16[8,128,256]{2,1,0:T(8,128)(2,1)}), bf16[8,128,256]{2,1,0:T(8,128)(2,1)S(1)}, u32[]{:S(2)}, u32[]{:S(2)}) async-start(bf16[8,128,256]{2,1,0:T(8,128)(2,1)} %bitcast.26), calls=%async_computation.5 | async-start | bytes 1048576 | tf_op jit(solution)/shard_map/all_to_all | solution.py:260
  137.2 1.1 copy.139
  138.3 7.7 %all-to-all-done.5 = bf16[8,128,256]{2,1,0:T(8,128)(2,1)S(1)} async-done(((bf16[8,128,256]{2,1,0:T(8,128)(2,1)}), bf16[8,128,256]{2,1,0:T(8,128)(2,1)S(1)}, u32[]{:S(2)}, u32[]{:S(2)}) %all-to-all-start.5) | async-done | bytes 524320 | tf_op jit(solution)/shard_map/all_to_all | solution.py:260
  146.0 0.1 slice_bitcast_fusion
  146.1 0.8 copy.147
  146.9 0.8 copy.148
  (52 shorter events, 0.9 us)
Async XLA Ops:
  0.6 1.0 copy-start
  0.6 8.1 %copy-start.11 = (f32[128,32]{0,1:T(8,128)S(1)}, f32[128,32]{0,1:T(8,128)}, u32[]{:S(2)}) copy-start(f32[128,32]{0,1:T(8,128)} %param.12) | copy-start | bytes 49156
  0.7 8.2 %copy-start.4 = (bf16[128,4096]{1,0:T(8,128)(2,1)S(1)}, bf16[128,4096]{1,0:T(8,128)(2,1)}, u32[]{:S(2)}) copy-start(bf16[128,4096]{1,0:T(8,128)(2,1)} %param.7) | copy-start | bytes 3145732
  3.5 14.2 %all-to-all-start.2 = ((bf16[8,128,256]{2,1,0:T(8,128)(2,1)}), bf16[8,128,256]{2,1,0:T(8,128)(2,1)}, u32[]{:S(2)}, u32[]{:S(2)}) async-start(bf16[8,128,256]{2,1,0:T(8,128)(2,1)} %maximum_bitcast_fusion.3), calls=%async_computation.2 | async-start | bytes 1048576 | tf_op jit(solution)/shard_map/all_to_all | solution.py:176
  8.8 1.6 %copy-start.1 = (bf16[128,4096]{1,0:T(8,128)(2,1)S(1)}, bf16[128,4096]{1,0:T(8,128)(2,1)}, u32[]{:S(2)}) copy-start(bf16[128,4096]{1,0:T(8,128)(2,1)} %param.11) | copy-start | bytes 3145732
  11.1 1.4 copy-start.6
  17.7 19.4 %all-to-all-start.1 = ((bf16[8,136,512]{2,1,0:T(8,128)(2,1)}), bf16[8,136,512]{2,1,0:T(8,128)(2,1)S(1)}, u32[]{:S(2)}, u32[]{:S(2)}) async-start(bf16[8,136,512]{2,1,0:T(8,128)(2,1)} %pad_maximum_fusion.1), calls=%async_computation.1 | async-start | bytes 2228224 | tf_op jit(solution)/shard_map/all_to_all | solution.py:189
  22.5 18.1 %copy-start.8 = (s32[4096]{0:T(1024)S(1)}, s32[4096]{0:T(1024)}, u32[]{:S(2)}) copy-start(s32[4096]{0:T(1024)} %param.13) | copy-start | bytes 49156
  37.1 29.1 %copy-start.2 = (bf16[8,136,512]{2,1,0:T(8,128)(2,1)}, bf16[8,136,512]{2,1,0:T(8,128)(2,1)S(1)}, u32[]{:S(2)}) copy-start(bf16[8,136,512]{2,1,0:T(8,128)(2,1)S(1)} %all-to-all-done.1.bulk_b) | copy-start | bytes 3342340
  37.1 18.7 %all-to-all-start = ((bf16[8,136,512]{2,1,0:T(8,128)(2,1)}), bf16[8,136,512]{2,1,0:T(8,128)(2,1)S(1)}, u32[]{:S(2)}, u32[]{:S(2)}) async-start(bf16[8,136,512]{2,1,0:T(8,128)(2,1)} %pad_maximum_fusion), calls=%async_computation | async-start | bytes 2228224 | tf_op jit(solution)/shard_map/all_to_all | solution.py:189
  42.3 14.2 %copy-start.12 = (s32[1024]{0:T(1024)}, s32[1024]{0:T(1024)S(1)}, u32[]{:S(2)}) copy-start(s32[1024]{0:T(1024)S(1)} %convert_reduce_fusion) | copy-start | bytes 12292
  43.8 22.4 %collective-permute-start = (bf16[512,256]{1,0:T(8,128)(2,1)S(1)}, bf16[512,256]{1,0:T(8,128)(2,1)}, u32[]{:S(2)}, u32[]{:S(2)}) collective-permute-start(bf16[512,256]{1,0:T(8,128)(2,1)S(1)} %bitcast.99), channel_id=1, source_target_pairs={{0,16},{8,24},{1,17},{9,25},{2,18},{10,26},{3,19},{11,27},{4,20},{... | collective-permute-start | bytes 786440 | tf_op jit(solution)/shard_map/ppermute | solution.py:197
  49.3 16.9 %collective-permute-start.1 = (bf16[1024,256]{1,0:T(8,128)(2,1)}, bf16[1024,256]{1,0:T(8,128)(2,1)S(1)}, u32[]{:S(2)}, u32[]{:S(2)}) collective-permute-start(bf16[1024,256]{1,0:T(8,128)(2,1)} %bitcast.18.kv_ref), channel_id=1, source_target_pairs={{0,8},{8,16},{16,24},{1,9},{9,17},{17,25},{2,10},{10,18},{18,26},{... | collective-permute-start | bytes 1572872 | tf_op jit(solution)/shard_map/ppermute | solution.py:197
  55.7 1.0 copy-start.3
  55.8 10.4 %copy-start.9 = (f32[4,1024]{1,0:T(4,128)}, f32[4,1024]{1,0:T(4,128)S(1)}, u32[]{:S(2)}) copy-start(f32[4,1024]{1,0:T(4,128)S(1)} %fusion.13.stat_ref) | copy-start | bytes 49156
  55.8 0.9 copy-start.10
  72.4 14.3 %copy-start.7 = (bf16[1536,256]{1,0:T(8,128)(2,1)S(1)}, bf16[1536,256]{1,0:T(8,128)(2,1)}, u32[]{:S(2)}) copy-start(bf16[1536,256]{1,0:T(8,128)(2,1)} %get-tuple-element.16) | copy-start | bytes 2359300
  82.8 48.5 %copy-start.5 = (f32[1024,256]{1,0:T(8,128)S(1)}, f32[1024,256]{1,0:T(8,128)}, u32[]{:S(2)}) copy-start(f32[1024,256]{1,0:T(8,128)} %get-tuple-element.15) | copy-start | bytes 3145732
  82.8 12.7 %all-to-all-start.4 = ((bf16[8,128,256]{2,1,0:T(8,128)(2,1)}), bf16[8,128,256]{2,1,0:T(8,128)(2,1)S(1)}, u32[]{:S(2)}, u32[]{:S(2)}) async-start(bf16[8,128,256]{2,1,0:T(8,128)(2,1)} %bitcast.98), calls=%async_computation.4 | async-start | bytes 1048576 | tf_op jit(solution)/shard_map/all_to_all | solution.py:256
  87.6 43.8 %collective-permute-start.2 = (bf16[1024,256]{1,0:T(8,128)(2,1)}, bf16[1024,256]{1,0:T(8,128)(2,1)}, u32[]{:S(2)}, u32[]{:S(2)}) collective-permute-start(bf16[1024,256]{1,0:T(8,128)(2,1)} %slice.84), channel_id=1, source_target_pairs={{8,0},{16,8},{24,16},{9,1},{17,9},{25,17},{10,2},{18,10},{26,18},{... | collective-permute-start | bytes 1572872 | tf_op jit(solution)/shard_map/ppermute | solution.py:244
  88.9 42.5 %collective-permute-start.3 = (bf16[512,256]{1,0:T(8,128)(2,1)S(1)}, bf16[512,256]{1,0:T(8,128)(2,1)S(1)}, u32[]{:S(2)}, u32[]{:S(2)}) collective-permute-start(bf16[512,256]{1,0:T(8,128)(2,1)S(1)} %slice.85), channel_id=1, source_target_pairs={{16,0},{24,8},{17,1},{25,9},{18,2},{26,10},{19,3},{27,11},{20,4},{... | collective-permute-start | bytes 786440 | tf_op jit(solution)/shard_map/ppermute | solution.py:244
  95.6 37.8 %all-to-all-start.3 = ((bf16[8,128,256]{2,1,0:T(8,128)(2,1)}), bf16[8,128,256]{2,1,0:T(8,128)(2,1)S(1)}, u32[]{:S(2)}, u32[]{:S(2)}) async-start(bf16[8,128,256]{2,1,0:T(8,128)(2,1)} %bitcast.97), calls=%async_computation.3 | async-start | bytes 1048576 | tf_op jit(solution)/shard_map/all_to_all | solution.py:248
  133.3 12.7 %all-to-all-start.5 = ((bf16[8,128,256]{2,1,0:T(8,128)(2,1)}), bf16[8,128,256]{2,1,0:T(8,128)(2,1)S(1)}, u32[]{:S(2)}, u32[]{:S(2)}) async-start(bf16[8,128,256]{2,1,0:T(8,128)(2,1)} %bitcast.26), calls=%async_computation.5 | async-start | bytes 1048576 | tf_op jit(solution)/shard_map/all_to_all | solution.py:260

commit v2 on v1

--- a/solution.py
+++ b/solution.py
@@ -103,24 +103,34 @@
     sweep(get, low_ref, stat_ref, start_ref, kv_ref, dq_t, dkv, window, window, lambda q0: None)
 
 
-def far_kernel(
-    tokens, low_ref, bulk_a, bulk_b, stat_ref, start_ref, kv_ref, dq_near, dq_out, dq_rest, dkv_out, dq_t, dkv
-):
-    d = HEAD_SIZE
+def far_kernel(tokens, steps, low_ref, bulk_a, bulk_b, stat_ref, start_ref, *refs):
+    d = HEAD_SIZE
+    kv_parts, refs = refs[:steps], refs[steps:]
+    dq_near, dq_out, dq_rest, refs = refs[0], refs[1], refs[2], refs[3:]
+    dkv_parts, (dq_t, dkv, kv_all) = refs[:steps], refs[steps:]
     half = dq_near.shape[0]
     heads = dq_t.shape[0]
+    window = kv_all.shape[0]
     dq_t[:half] = dq_near[...]
     dq_t[half:] = jnp.zeros_like(dq_rest)
     dkv[...] = jnp.zeros_like(dkv)
+    at = window
+    for part in kv_parts:
+        at -= part.shape[0]
+        kv_all[at : at + part.shape[0], :] = part[...]
     get = getters([bulk_a, bulk_b], tokens)
 
     def finish(q0):
         write_dq(dq_t, range(half), dq_out, q0)
 
-    sweep(get, low_ref, stat_ref, start_ref, kv_ref, dq_t, dkv, 0, kv_ref.shape[0], finish)
+    sweep(get, low_ref, stat_ref, start_ref, kv_all, dq_t, dkv, 0, window, finish)
     dq_rest[...] = dq_t[half:heads]
-    dkv_out[:, :d] = (dkv[:, :d] * (1.0 / math.sqrt(d))).astype(dkv_out.dtype)
-    dkv_out[:, d:] = dkv[:, d:].astype(dkv_out.dtype)
+    at = window
+    for part in dkv_parts:
+        at -= part.shape[0]
+        cut = slice(at, at + part.shape[0])
+        part[:, :d] = (dkv[cut, :d] * (1.0 / math.sqrt(d))).astype(part.dtype)
+        part[:, d:] = dkv[cut, d:].astype(part.dtype)
 
 
 def late_kernel(
@@ -196,8 +206,6 @@
         arrived.append(
             lax.ppermute(kv[rows - sizes[by - 1] :], "outer", [(i, i + by) for i in range(outers - by)])
         )
-    kv_far = jnp.concatenate(arrived[::-1], axis=0)
-
     padded = jnp.concatenate([jnp.full((window,), -1, segment_ids.dtype), segment_ids])
     seg_keys = lax.dynamic_slice_in_dim(padded, place * rows, window + rows, 0)
     seg_query = seg_keys[window:]
@@ -229,21 +237,21 @@
         flops,
         *(low, bulk[0], stats[0], start, kv),
     )
-    dq_a, dq_far, dkv_far = call(
-        functools.partial(far_kernel, tokens),
-        (dq_done, dq_shape, jax.ShapeDtypeStruct((window, 2 * d), jnp.bfloat16)),
-        [pltpu.VMEM((heads, d, rows), jnp.float32), pltpu.VMEM((window, 2 * d), jnp.float32)],
+    dq_a, dq_far, *dkv_far = call(
+        functools.partial(far_kernel, tokens, steps),
+        (dq_done, dq_shape) + tuple(jax.ShapeDtypeStruct((size, 2 * d), jnp.bfloat16) for size in sizes),
+        [
+            pltpu.VMEM((heads, d, rows), jnp.float32),
+            pltpu.VMEM((window, 2 * d), jnp.float32),
+            pltpu.VMEM((window, 2 * d), jnp.bfloat16),
+        ],
         4 * flops,
-        *(low, bulk[0], bulk[1], jnp.concatenate(stats, axis=0), start, kv_far, dq_near),
+        *(low, bulk[0], bulk[1], jnp.concatenate(stats, axis=0), start, *arrived, dq_near),
     )
     returned = []
-    at = window
     for by in range(1, steps + 1):
-        at -= sizes[by - 1]
         returned.append(
-            lax.ppermute(
-                dkv_far[at : at + sizes[by - 1]], "outer", [(i + by, i) for i in range(outers - by)]
-            )
+            lax.ppermute(dkv_far[by - 1], "outer", [(i + by, i) for i in range(outers - by)])
         )
     dq_a = lax.all_to_all(dq_a.reshape(parts, tokens, half * d), GROUP, 0, 0)
     dq_b, dkv = call(

time: 149 us -> 146 us (0.980)
  other arithmetic: 10.3 us -> 7.34 us
    concatenate x1 -> x0, other arithmetic: 1.89 us -> none  [whole(): kv_far = jnp.concatenate(arrived[::-1], axis=0)]
    unnamed x35 -> x37, local copies, waits for them, and re-layouts: 6.59 us -> 7.38 us
  transfers between devices with their start and end apart: 10 -> 10, of which waited for: 5 -> 5; matrix products, arithmetic and copies ran while one was open for 12% -> 11% of each run, Pallas kernels for 6% -> 7%
where the time goes in v2:
time: 146 us; the launch traced here: 145 us
  waiting for transfers between devices  61.6 us (42%)
  starting transfers between devices  35.8 us (25%)
  Pallas kernels  24.1 us (17%)
  local copies, waits for them, and re-layouts  14.8 us (10%)
  other arithmetic  7.34 us (5%)
    ppermute x2, waiting for transfers between devices, whole(): lax.ppermute(dkv_far[by - 1], 'outer', [(i + by, i) for i in range(outers...  31.4 us
    pallas_call x3, Pallas kernels, call(): pl.pallas_call(kernel, out_shape=out_shape, in_specs=[smem] + [vmem] * (l...  24.1 us
    all_to_all x2, waiting for transfers between devices, whole(): bulk.append(lax.all_to_all(sent, GROUP, 0, 0))  16.2 us
    ppermute x2, starting transfers between devices, whole(): lax.ppermute(kv[rows - sizes[by - 1]:], 'outer', [(i, i + by) for i in ra...  9.04 us
    all_to_all x2, starting transfers between devices, whole(): bulk.append(lax.all_to_all(sent, GROUP, 0, 0))  7.76 us
    all_to_all x1, waiting for transfers between devices, whole(): lax.all_to_all(dkv.astype(jnp.bfloat16).reshape(parts, tokens, 2 * d), GR...  7.69 us
    unnamed x37, local copies, waits for them, and re-layouts  7.38 us
    all_to_all x1, waiting for transfers between devices, whole(): dq_b = lax.all_to_all(dq_b.reshape(parts, tokens, half * d), GROUP, 0, 0)  6.26 us
  transfers between devices with their start and end apart: 10, of which 5 were waited for; matrix products, arithmetic and copies ran while one was open for 11% of the time, Pallas kernels for 7%

profile of v2, /device:TPU:0, one launch (start us, length us, event | category | flops | bytes accessed | tf_op | source)
XLA Modules:
  0.0 144.7 jit_solution(4264871488088625621)
XLA Ops:
  0.7 0.9 copy-done
  1.6 1.1 copy_bitcast_fusion.2
  2.7 0.8 maximum_bitcast_fusion.3
  3.5 5.2 %all-to-all-start.2 = ((bf16[8,128,256]{2,1,0:T(8,128)(2,1)}), bf16[8,128,256]{2,1,0:T(8,128)(2,1)}, u32[]{:S(2)}, u32[]{:S(2)}) async-start(bf16[8,128,256]{2,1,0:T(8,128)(2,1)} %maximum_bitcast_fusion.3), calls=%async_computation.2 | async-start | bytes 1048576 | tf_op jit(solution)/shard_map/all_to_all | solution.py:186
  8.7 0.1 copy.108
  8.9 0.7 copy.104
  9.5 0.9 fusion.18
  10.4 0.7 copy.106
  11.1 0.9 fusion.19
  12.0 0.5 copy-done.6
  12.5 0.2 multiply_bitcast_fusion
  12.8 0.4 copy.142
  13.1 0.6 reduce_sum.19
  13.9 1.2 copy.129
  15.1 1.2 copy.130
  16.6 1.1 pad_maximum_fusion.1
  17.7 4.2 %all-to-all-start.1 = ((bf16[8,136,512]{2,1,0:T(8,128)(2,1)}), bf16[8,136,512]{2,1,0:T(8,128)(2,1)S(1)}, u32[]{:S(2)}, u32[]{:S(2)}) async-start(bf16[8,136,512]{2,1,0:T(8,128)(2,1)} %pad_maximum_fusion.1), calls=%async_computation.1 | async-start | bytes 2228224 | tf_op jit(solution)/shard_map/all_to_all | solution.py:199
  21.9 0.2 copy.127
  22.1 0.2 copy.128
  22.4 0.1 maximum_bitcast_fusion
  22.5 1.1 pad_maximum_fusion
  23.6 13.4 %all-to-all-done.1.bulk_b = bf16[8,136,512]{2,1,0:T(8,128)(2,1)S(1)} async-done(((bf16[8,136,512]{2,1,0:T(8,128)(2,1)}), bf16[8,136,512]{2,1,0:T(8,128)(2,1)S(1)}, u32[]{:S(2)}, u32[]{:S(2)}) %all-to-all-start.1) | async-done | bytes 1114144 | tf_op jit(solution)/shard_map/all_to_all | solution.py:199
  37.1 3.6 %all-to-all-start = ((bf16[8,136,512]{2,1,0:T(8,128)(2,1)}), bf16[8,136,512]{2,1,0:T(8,128)(2,1)S(1)}, u32[]{:S(2)}, u32[]{:S(2)}) async-start(bf16[8,136,512]{2,1,0:T(8,128)(2,1)} %pad_maximum_fusion), calls=%async_computation | async-start | bytes 2228224 | tf_op jit(solution)/shard_map/all_to_all | solution.py:199
  40.8 1.4 convert_reduce_fusion
  42.3 0.6 slice.61.low_ref
  42.9 1.0 slice.94
  43.8 5.5 %collective-permute-start.1 = (bf16[512,256]{1,0:T(8,128)(2,1)S(1)}, bf16[512,256]{1,0:T(8,128)(2,1)}, u32[]{:S(2)}, u32[]{:S(2)}) collective-permute-start(bf16[512,256]{1,0:T(8,128)(2,1)S(1)} %bitcast.98), channel_id=1, source_target_pairs={{0,16},{8,24},{1,17},{9,25},{2,18},{10,26},{3,19},{11,27},{4,20},{... | collective-permute-start | bytes 786440 | tf_op jit(solution)/shard_map/ppermute | solution.py:207
  49.4 3.5 %collective-permute-start = (bf16[1024,256]{1,0:T(8,128)(2,1)}, bf16[1024,256]{1,0:T(8,128)(2,1)S(1)}, u32[]{:S(2)}, u32[]{:S(2)}) collective-permute-start(bf16[1024,256]{1,0:T(8,128)(2,1)} %bitcast.17.kv_ref), channel_id=1, source_target_pairs={{0,8},{8,16},{16,24},{1,9},{9,17},{17,25},{2,10},{10,18},{18,26},{... | collective-permute-start | bytes 1572872 | tf_op jit(solution)/shard_map/ppermute | solution.py:207
  52.9 2.8 %all-to-all-done.bulk_a = bf16[8,136,512]{2,1,0:T(8,128)(2,1)S(1)} async-done(((bf16[8,136,512]{2,1,0:T(8,128)(2,1)}), bf16[8,136,512]{2,1,0:T(8,128)(2,1)S(1)}, u32[]{:S(2)}, u32[]{:S(2)}) %all-to-all-start) | async-done | bytes 1114144 | tf_op jit(solution)/shard_map/all_to_all | solution.py:199
  55.9 0.6 pad_maximum_fusion.3.stat_ref
  56.5 0.3 copy-done.3
  56.7 9.4 %shard_map.94 = (f32[2,128,1024]{2,1,0:T(8,128)}, f32[1024,256]{1,0:T(8,128)}) custom-call(s32[4]{0:T(128)} %slice.61.low_ref, bf16[8,136,512]{2,1,0:T(8,128)(2,1)} %copy-done.3, f32[4,1024]{1,0:T(4,128)} %copy-done.9, s32[1,1024]{1,0:T(1,128)} %bitcast.103, bf16[1024,256]{1,0:T(8,128)(2,1)} %bitcast.17.kv_ref), custom_call_target="tpu_custom_call" | custom-call | flops 1342177280 | bytes 4194304 | tf_op jit(solution)/shard_map/pallas_call | solution.py:224
  66.2 0.8 copy-done.11
  67.0 4.3 %shard_map.95 = (bf16[1024,256]{1,0:T(8,128)(2,1)}, f32[2,128,1024]{2,1,0:T(8,128)}, bf16[1024,256]{1,0:T(8,128)(2,1)}, bf16[512,256]{1,0:T(8,128)(2,1)}) custom-call(s32[4]{0:T(128)} %slice.61.low_ref, bf16[8,136,512]{2,1,0:T(8,128)(2,1)} %copy-done.3, bf16[8,136,512]{2,1,0:T(8,128)(2,1)} %copy-done.2, f32[8,1024]{1,0:T(8,128)} %pad_maximum_fusion.3.stat_ref, ...), custom_call_target="tpu_custom_call" | custom-call | flops 5368709120 | bytes 4194304 | tf_op jit(solution)/shard_map/pallas_call | solution.py:224
  71.3 10.3 %shard_map.96 = (bf16[1024,256]{1,0:T(8,128)(2,1)}, f32[1024,256]{1,0:T(8,128)}) custom-call(s32[4]{0:T(128)} %slice.61.low_ref, bf16[8,136,512]{2,1,0:T(8,128)(2,1)} %copy-done.2, f32[4,1024]{1,0:T(4,128)} %copy-done.8, s32[1,1024]{1,0:T(1,128)} %bitcast.105, bf16[1024,256]{1,0:T(8,128)(2,1)} %bitcast.17.kv_ref, f32[2,128,1024]{2,1,0:T(8,128)} %get-tuple-element.13.dq_far, ...), custom_call_target="tpu_custom_call" | custom-call | flops 1342177280 | bytes 4194304 | tf_op jit(solution)/shard_map/pallas_call | solution.py:224
  81.7 3.9 %all-to-all-start.4 = ((bf16[8,128,256]{2,1,0:T(8,128)(2,1)}), bf16[8,128,256]{2,1,0:T(8,128)(2,1)S(1)}, u32[]{:S(2)}, u32[]{:S(2)}) async-start(bf16[8,128,256]{2,1,0:T(8,128)(2,1)} %bitcast.97), calls=%async_computation.4 | async-start | bytes 1048576 | tf_op jit(solution)/shard_map/all_to_all | solution.py:264
  85.6 1.3 collective-permute-start.2
  86.9 1.3 collective-permute-start.3
  88.2 6.3 %all-to-all-done.4 = bf16[8,128,256]{2,1,0:T(8,128)(2,1)S(1)} async-done(((bf16[8,128,256]{2,1,0:T(8,128)(2,1)}), bf16[8,128,256]{2,1,0:T(8,128)(2,1)S(1)}, u32[]{:S(2)}, u32[]{:S(2)}) %all-to-all-start.4) | async-done | bytes 524320 | tf_op jit(solution)/shard_map/all_to_all | solution.py:264
  94.5 3.5 %all-to-all-start.3 = ((bf16[8,128,256]{2,1,0:T(8,128)(2,1)}), bf16[8,128,256]{2,1,0:T(8,128)(2,1)S(1)}, u32[]{:S(2)}, u32[]{:S(2)}) async-start(bf16[8,128,256]{2,1,0:T(8,128)(2,1)} %bitcast.21), calls=%async_computation.3 | async-start | bytes 1048576 | tf_op jit(solution)/shard_map/all_to_all | solution.py:256
  98.0 31.4 %collective-permute-done.3 = bf16[512,256]{1,0:T(8,128)(2,1)S(1)} collective-permute-done((bf16[512,256]{1,0:T(8,128)(2,1)S(1)}, bf16[512,256]{1,0:T(8,128)(2,1)S(1)}, u32[]{:S(2)}, u32[]{:S(2)}) %collective-permute-start.3) | collective-permute-done | bytes 262176 | tf_op jit(solution)/shard_map/ppermute | solution.py:254
  129.4 0.9 add_convert_fusion
  130.3 3.8 %all-to-all-start.5 = ((bf16[8,128,256]{2,1,0:T(8,128)(2,1)}), bf16[8,128,256]{2,1,0:T(8,128)(2,1)S(1)}, u32[]{:S(2)}, u32[]{:S(2)}) async-start(bf16[8,128,256]{2,1,0:T(8,128)(2,1)} %bitcast.26), calls=%async_computation.5 | async-start | bytes 1048576 | tf_op jit(solution)/shard_map/all_to_all | solution.py:268
  134.2 1.1 copy.139
  135.3 7.7 %all-to-all-done.5 = bf16[8,128,256]{2,1,0:T(8,128)(2,1)S(1)} async-done(((bf16[8,128,256]{2,1,0:T(8,128)(2,1)}), bf16[8,128,256]{2,1,0:T(8,128)(2,1)S(1)}, u32[]{:S(2)}, u32[]{:S(2)}) %all-to-all-start.5) | async-done | bytes 524320 | tf_op jit(solution)/shard_map/all_to_all | solution.py:268
  143.0 0.1 slice_bitcast_fusion
  143.1 0.8 copy.147
  143.9 0.8 copy.148
  (51 shorter events, 0.8 us)
Async XLA Ops:
  0.6 1.0 copy-start
  0.6 8.1 %copy-start.10 = (f32[128,32]{0,1:T(8,128)S(1)}, f32[128,32]{0,1:T(8,128)}, u32[]{:S(2)}) copy-start(f32[128,32]{0,1:T(8,128)} %param.12) | copy-start | bytes 49156
  0.7 8.2 %copy-start.4 = (bf16[128,4096]{1,0:T(8,128)(2,1)S(1)}, bf16[128,4096]{1,0:T(8,128)(2,1)}, u32[]{:S(2)}) copy-start(bf16[128,4096]{1,0:T(8,128)(2,1)} %param.7) | copy-start | bytes 3145732
  3.5 14.2 %all-to-all-start.2 = ((bf16[8,128,256]{2,1,0:T(8,128)(2,1)}), bf16[8,128,256]{2,1,0:T(8,128)(2,1)}, u32[]{:S(2)}, u32[]{:S(2)}) async-start(bf16[8,128,256]{2,1,0:T(8,128)(2,1)} %maximum_bitcast_fusion.3), calls=%async_computation.2 | async-start | bytes 1048576 | tf_op jit(solution)/shard_map/all_to_all | solution.py:186
  8.8 1.6 %copy-start.1 = (bf16[128,4096]{1,0:T(8,128)(2,1)S(1)}, bf16[128,4096]{1,0:T(8,128)(2,1)}, u32[]{:S(2)}) copy-start(bf16[128,4096]{1,0:T(8,128)(2,1)} %param.11) | copy-start | bytes 3145732
  11.1 1.4 copy-start.6
  17.7 19.4 %all-to-all-start.1 = ((bf16[8,136,512]{2,1,0:T(8,128)(2,1)}), bf16[8,136,512]{2,1,0:T(8,128)(2,1)S(1)}, u32[]{:S(2)}, u32[]{:S(2)}) async-start(bf16[8,136,512]{2,1,0:T(8,128)(2,1)} %pad_maximum_fusion.1), calls=%async_computation.1 | async-start | bytes 2228224 | tf_op jit(solution)/shard_map/all_to_all | solution.py:199
  22.5 18.1 %copy-start.7 = (s32[4096]{0:T(1024)S(1)}, s32[4096]{0:T(1024)}, u32[]{:S(2)}) copy-start(s32[4096]{0:T(1024)} %param.13) | copy-start | bytes 49156
  37.1 29.1 %copy-start.2 = (bf16[8,136,512]{2,1,0:T(8,128)(2,1)}, bf16[8,136,512]{2,1,0:T(8,128)(2,1)S(1)}, u32[]{:S(2)}) copy-start(bf16[8,136,512]{2,1,0:T(8,128)(2,1)S(1)} %all-to-all-done.1.bulk_b) | copy-start | bytes 3342340
  37.1 18.7 %all-to-all-start = ((bf16[8,136,512]{2,1,0:T(8,128)(2,1)}), bf16[8,136,512]{2,1,0:T(8,128)(2,1)S(1)}, u32[]{:S(2)}, u32[]{:S(2)}) async-start(bf16[8,136,512]{2,1,0:T(8,128)(2,1)} %pad_maximum_fusion), calls=%async_computation | async-start | bytes 2228224 | tf_op jit(solution)/shard_map/all_to_all | solution.py:199
  42.3 14.2 %copy-start.13 = (s32[1024]{0:T(1024)}, s32[1024]{0:T(1024)S(1)}, u32[]{:S(2)}) copy-start(s32[1024]{0:T(1024)S(1)} %convert_reduce_fusion) | copy-start | bytes 12292
  43.8 22.4 %collective-permute-start.1 = (bf16[512,256]{1,0:T(8,128)(2,1)S(1)}, bf16[512,256]{1,0:T(8,128)(2,1)}, u32[]{:S(2)}, u32[]{:S(2)}) collective-permute-start(bf16[512,256]{1,0:T(8,128)(2,1)S(1)} %bitcast.98), channel_id=1, source_target_pairs={{0,16},{8,24},{1,17},{9,25},{2,18},{10,26},{3,19},{11,27},{4,20},{... | collective-permute-start | bytes 786440 | tf_op jit(solution)/shard_map/ppermute | solution.py:207
  49.4 16.8 %collective-permute-start = (bf16[1024,256]{1,0:T(8,128)(2,1)}, bf16[1024,256]{1,0:T(8,128)(2,1)S(1)}, u32[]{:S(2)}, u32[]{:S(2)}) collective-permute-start(bf16[1024,256]{1,0:T(8,128)(2,1)} %bitcast.17.kv_ref), channel_id=1, source_target_pairs={{0,8},{8,16},{16,24},{1,9},{9,17},{17,25},{2,10},{10,18},{18,26},{... | collective-permute-start | bytes 1572872 | tf_op jit(solution)/shard_map/ppermute | solution.py:207
  55.7 1.0 copy-start.3
  55.8 10.4 %copy-start.8 = (f32[4,1024]{1,0:T(4,128)}, f32[4,1024]{1,0:T(4,128)S(1)}, u32[]{:S(2)}) copy-start(f32[4,1024]{1,0:T(4,128)S(1)} %fusion.13.stat_ref) | copy-start | bytes 49156
  55.8 0.9 copy-start.9
  66.2 0.8 copy-start.11
  71.3 15.6 %copy-start.12 = (bf16[512,256]{1,0:T(8,128)(2,1)S(1)}, bf16[512,256]{1,0:T(8,128)(2,1)}, u32[]{:S(2)}) copy-start(bf16[512,256]{1,0:T(8,128)(2,1)} %get-tuple-element.18) | copy-start | bytes 786436
  81.7 47.7 %copy-start.5 = (f32[1024,256]{1,0:T(8,128)S(1)}, f32[1024,256]{1,0:T(8,128)}, u32[]{:S(2)}) copy-start(f32[1024,256]{1,0:T(8,128)} %get-tuple-element.16) | copy-start | bytes 3145732
  81.7 12.8 %all-to-all-start.4 = ((bf16[8,128,256]{2,1,0:T(8,128)(2,1)}), bf16[8,128,256]{2,1,0:T(8,128)(2,1)S(1)}, u32[]{:S(2)}, u32[]{:S(2)}) async-start(bf16[8,128,256]{2,1,0:T(8,128)(2,1)} %bitcast.97), calls=%async_computation.4 | async-start | bytes 1048576 | tf_op jit(solution)/shard_map/all_to_all | solution.py:264
  85.6 43.8 %collective-permute-start.2 = (bf16[1024,256]{1,0:T(8,128)(2,1)}, bf16[1024,256]{1,0:T(8,128)(2,1)S(1)}, u32[]{:S(2)}, u32[]{:S(2)}) collective-permute-start(bf16[1024,256]{1,0:T(8,128)(2,1)} %get-tuple-element.17), channel_id=1, source_target_pairs={{8,0},{16,8},{24,16},{9,1},{17,9},{25,17},{10,2},{18,10},{26,18},{... | collective-permute-start | bytes 1572872 | tf_op jit(solution)/shard_map/ppermute | solution.py:254
  86.9 42.5 %collective-permute-start.3 = (bf16[512,256]{1,0:T(8,128)(2,1)S(1)}, bf16[512,256]{1,0:T(8,128)(2,1)S(1)}, u32[]{:S(2)}, u32[]{:S(2)}) collective-permute-start(bf16[512,256]{1,0:T(8,128)(2,1)S(1)} %copy-done.12), channel_id=1, source_target_pairs={{16,0},{24,8},{17,1},{25,9},{18,2},{26,10},{19,3},{27,11},{20,4},{... | collective-permute-start | bytes 786440 | tf_op jit(solution)/shard_map/ppermute | solution.py:254
  94.5 35.9 %all-to-all-start.3 = ((bf16[8,128,256]{2,1,0:T(8,128)(2,1)}), bf16[8,128,256]{2,1,0:T(8,128)(2,1)S(1)}, u32[]{:S(2)}, u32[]{:S(2)}) async-start(bf16[8,128,256]{2,1,0:T(8,128)(2,1)} %bitcast.21), calls=%async_computation.3 | async-start | bytes 1048576 | tf_op jit(solution)/shard_map/all_to_all | solution.py:256
  130.3 12.7 %all-to-all-start.5 = ((bf16[8,128,256]{2,1,0:T(8,128)(2,1)}), bf16[8,128,256]{2,1,0:T(8,128)(2,1)S(1)}, u32[]{:S(2)}, u32[]{:S(2)}) async-start(bf16[8,128,256]{2,1,0:T(8,128)(2,1)} %bitcast.26), calls=%async_computation.5 | async-start | bytes 1048576 | tf_op jit(solution)/shard_map/all_to_all | solution.py:268
